TPU v7x, 32 devices: a 4x2x2 block of a 4x4x8 slice. The times are simulated.
32 devices in a mesh: dp: 4 (over y, z), wg: 8 (over x, core).
Axes of the slice: x: 4, y: 2, z: 2, core: 2. Of those that a mesh axis runs over, the one named last changes fastest.
The devices are a block of a 4x4x8 slice.
Arguments:
- hidden: bfloat16 [32768, 1024], P(('dp', 'wg')), parts along dimension 0
- choice: int32 [32768, 8], P(('dp', 'wg')), parts along dimension 0
- pre_scale: float32 [1024], replicated
- w_router: bfloat16 [1024, 32], replicated
- w_gelu: bfloat16 [32, 1024, 512], P(None, None, 'wg')
- w_linear: bfloat16 [32, 1024, 512], P(None, None, 'wg')
- w_down: bfloat16 [32, 512, 1024], P(None, 'wg')
- post_scale: float32 [1024], replicated
Outputs:
- output: bfloat16 [32768, 1024], P(('dp', 'wg')), parts along dimension 0
There are 4 independent parts. A program takes and returns all parts, laid end to end along the dimension named above; an argument that names none is the same for every part.
All inputs are finite; a program needn't handle non-finite values.
Results may differ from a plain program's by a relative error of at most 0.001.
Values are sent between devices in bfloat16 or wider.
A program may use at most 768 MiB of HBM per device.

v0:
```python
import jax
import jax.numpy as jnp
from jax import lax
from jax.sharding import PartitionSpec as P

EPS = 1e-5


def rms_norm(values, gain_vec):
    return values * lax.rsqrt(jnp.mean(values * values, axis=-1, keepdims=True) + EPS) * gain_vec


def route_slots(block_ids, num_experts, capacity):
    tok_rows, top_k = block_ids.shape
    flat_ids = block_ids.reshape(-1)
    sort_order = jnp.argsort(flat_ids, stable=True)
    counts = jnp.sum((flat_ids[:, None] == jnp.arange(num_experts)[None, :]).astype(jnp.int32), axis=0)
    starts = jnp.cumsum(counts) - counts
    slot_rank = jnp.arange(capacity)
    source = jnp.minimum(starts[:, None] + slot_rank[None, :], tok_rows * top_k - 1)
    slot_token = sort_order[source].reshape(-1) // top_k
    sorted_pos = jnp.argsort(sort_order, stable=True)
    slot_of = flat_ids * capacity + sorted_pos - starts[flat_ids]
    return slot_token, slot_of


def solution(mesh):
    def local_block(hidden, choice, pre_scale, w_router, w_gelu, w_linear, w_down, post_scale):
        tok_rows, d_model = hidden.shape
        num_experts = w_gelu.shape[0]
        top_k = choice.shape[1]
        capacity = 2 * tok_rows * top_k // num_experts
        hidden_f = hidden.astype(jnp.float32)
        normed = rms_norm(hidden_f, pre_scale).astype(jnp.bfloat16)
        router_probs = jax.nn.softmax(jnp.dot(normed, w_router, preferred_element_type=jnp.float32), axis=-1)
        gate_vals = jnp.take_along_axis(router_probs, choice, axis=1)
        slot_token, slot_of = route_slots(choice, num_experts, capacity)
        dispatched = jnp.take(normed, slot_token, axis=0).reshape(num_experts, capacity, d_model)

        def one_expert(expert_args):
            expert_rows, gelu_part, linear_part, down_part = expert_args
            gelu_full = lax.all_gather(gelu_part, 'wg', axis=1, tiled=True)
            linear_full = lax.all_gather(linear_part, 'wg', axis=1, tiled=True)
            down_full = lax.all_gather(down_part, 'wg', axis=0, tiled=True)
            gelu_in = jnp.dot(expert_rows, gelu_full, preferred_element_type=jnp.float32)
            linear_in = jnp.dot(expert_rows, linear_full, preferred_element_type=jnp.float32)
            hidden_act = (jax.nn.gelu(gelu_in, approximate=True) * linear_in).astype(jnp.bfloat16)
            return jnp.dot(hidden_act, down_full, preferred_element_type=jnp.float32)

        expert_out = lax.map(one_expert, (dispatched, w_gelu, w_linear, w_down)).reshape(num_experts * capacity, d_model)
        picked = jnp.take(expert_out, slot_of, axis=0).reshape(tok_rows, top_k, d_model)
        mixed_out = jnp.sum(picked * gate_vals[:, :, None], axis=1)
        return (hidden_f + rms_norm(mixed_out, post_scale)).astype(jnp.bfloat16)

    row_spec = P(('dp', 'wg'), None)
    weight_in = P(None, None, 'wg')
    return jax.shard_map(local_block, mesh=mesh, in_specs=(row_spec, row_spec, P(), P(), weight_in, weight_in, P(None, 'wg', None), P()), out_specs=row_spec, check_vma=False)
```

profile of v0, /device:TPU:81, one launch (start us, length us, event | category | flops | bytes accessed | tf_op | source)
XLA Modules:
  0.0 2732.6 jit_solution(7602965906206629295)
XLA Ops:
  31.6 90.7 %gather_fusion = s32[16384]{0:T(1024)S(1)} fusion(s32[8192]{0:T(1024)S(1)} %get-tuple-element.39, s32[16384]{0:T(1024)S(1)} %broadcast_clamp_fusion.1), kind=kCustom, calls=%fused_computation | custom fusion | bytes 196608 | tf_op jit(solution)/shard_map/gather | solution.py:21
  146.0 65.5 %gather_fusion.3 = f32[8192]{0:T(1024)S(1)} fusion(f32[1024,32]{0,1:T(8,128)S(1)} %fusion.37, s32[8192]{0:T(1024)S(1)} %reshape.307), kind=kCustom, calls=%fused_computation.3 | custom fusion | bytes 131072 | tf_op jit(solution)/shard_map/jit(take_along_axis)/gather | solution.py:36
  213.0 82.1 %gather_fusion.1 = bf16[16384,1024]{1,0:T(8,128)(2,1)} fusion(bf16[1024,1024]{1,0:T(8,128)(2,1)} %copy-done.2, s32[16384]{0:T(1024)S(1)} %copy-done.8), kind=kCustom, calls=%fused_computation.1 | custom fusion | bytes 67174400 | tf_op jit(solution)/shard_map/jit(_take)/gather | solution.py:38
  295.1 22.8 broadcast_select_fusion
  317.9 2232.3 %while.10 = (s32[]{:T(128)}, f32[32,512,1024]{2,1,0:T(8,128)}, bf16[32,512,1024]{2,1,0:T(8,128)(2,1)}, bf16[32,1024,64]{1,2,0:T(8,128)(2,1)}, bf16[32,1024,64]{1...) while((s32[]{:T(128)}, f32[32,512,1024]{2,1,0:T(8,128)}, bf16[32,512,1024]{2,1,0:T(8,128)(2,1)}, ...), condition=%wide.region_6.7_spmd, body=%wide.region_5.6_spmd.sunk | while | flops 1613234176 | bytes 20841692 | solution.py:50
  323.0 21.9 all-gather.13.cloned.1.call-done
  366.4 21.5 all-gather.17.cloned.1.call-done
  435.9 21.3 all-gather.17.cloned.1.call-done
  505.6 21.5 all-gather.17.cloned.1.call-done
  575.2 21.3 all-gather.17.cloned.1.call-done
  644.8 21.3 all-gather.17.cloned.1.call-done
  714.1 21.3 all-gather.17.cloned.1.call-done
  783.7 21.5 all-gather.17.cloned.1.call-done
  853.6 21.3 all-gather.17.cloned.1.call-done
  923.3 21.3 all-gather.17.cloned.1.call-done
  1201.9 21.3 all-gather.17.cloned.1.call-done
  1271.7 21.5 all-gather.17.cloned.1.call-done
  1341.3 21.3 all-gather.17.cloned.1.call-done
  1480.0 21.3 all-gather.17.cloned.1.call-done
  1549.6 21.5 all-gather.17.cloned.1.call-done
  1619.5 21.5 all-gather.17.cloned.1.call-done
  1688.9 21.5 all-gather.17.cloned.1.call-done
  1828.2 21.3 all-gather.17.cloned.1.call-done
  1897.6 21.5 all-gather.17.cloned.1.call-done
  1967.3 21.3 all-gather.17.cloned.1.call-done
  2036.5 21.5 all-gather.17.cloned.1.call-done
  2106.1 21.5 all-gather.17.cloned.1.call-done
  2176.0 21.5 all-gather.17.cloned.1.call-done
  2245.6 21.3 all-gather.17.cloned.1.call-done
  2384.6 21.5 all-gather.17.cloned.1.call-done
  2524.1 21.5 all-gather.17.cloned.1.call-done
  2550.2 153.8 %gather_fusion.2 = f32[8192,1024]{1,0:T(8,128)} fusion(f32[16384,1024]{1,0:T(8,128)} %bitcast.42, s32[8192]{0:T(1024)S(1)} %copy-done.9), kind=kCustom, calls=%fused_computation.2 | custom fusion | bytes 67141632 | tf_op jit(solution)/shard_map/jit(_take)/gather | solution.py:51
  (492 shorter events, 1745.4 us)
Async XLA Ops:
  321.3 66.6 %all-gather.17.cloned.1.call-start = ((), (), s32[]{:S(2)}) async-start(), calls=%async_computation.2 | async-start | bytes 1179648 | tf_op jit(solution)/shard_map/while/body/eval_jaxpr/all_gather | solution.py:43
  395.9 61.3 %all-gather.17.cloned.1.call-start = ((), (), s32[]{:S(2)}) async-start(), calls=%async_computation.2 | async-start | bytes 1179648 | tf_op jit(solution)/shard_map/while/body/eval_jaxpr/all_gather | solution.py:43
  465.1 61.9 %all-gather.17.cloned.1.call-start = ((), (), s32[]{:S(2)}) async-start(), calls=%async_computation.2 | async-start | bytes 1179648 | tf_op jit(solution)/shard_map/while/body/eval_jaxpr/all_gather | solution.py:43
  535.0 61.5 %all-gather.17.cloned.1.call-start = ((), (), s32[]{:S(2)}) async-start(), calls=%async_computation.2 | async-start | bytes 1179648 | tf_op jit(solution)/shard_map/while/body/eval_jaxpr/all_gather | solution.py:43
  604.5 61.6 %all-gather.17.cloned.1.call-start = ((), (), s32[]{:S(2)}) async-start(), calls=%async_computation.2 | async-start | bytes 1179648 | tf_op jit(solution)/shard_map/while/body/eval_jaxpr/all_gather | solution.py:43
  674.2 61.3 %all-gather.17.cloned.1.call-start = ((), (), s32[]{:S(2)}) async-start(), calls=%async_computation.2 | async-start | bytes 1179648 | tf_op jit(solution)/shard_map/while/body/eval_jaxpr/all_gather | solution.py:43
  743.4 61.8 %all-gather.17.cloned.1.call-start = ((), (), s32[]{:S(2)}) async-start(), calls=%async_computation.2 | async-start | bytes 1179648 | tf_op jit(solution)/shard_map/while/body/eval_jaxpr/all_gather | solution.py:43
  813.2 61.8 %all-gather.17.cloned.1.call-start = ((), (), s32[]{:S(2)}) async-start(), calls=%async_computation.2 | async-start | bytes 1179648 | tf_op jit(solution)/shard_map/while/body/eval_jaxpr/all_gather | solution.py:43
  883.0 61.6 %all-gather.17.cloned.1.call-start = ((), (), s32[]{:S(2)}) async-start(), calls=%async_computation.2 | async-start | bytes 1179648 | tf_op jit(solution)/shard_map/while/body/eval_jaxpr/all_gather | solution.py:43
  952.6 61.8 %all-gather.17.cloned.1.call-start = ((), (), s32[]{:S(2)}) async-start(), calls=%async_computation.2 | async-start | bytes 1179648 | tf_op jit(solution)/shard_map/while/body/eval_jaxpr/all_gather | solution.py:43
  1022.3 61.8 %all-gather.17.cloned.1.call-start = ((), (), s32[]{:S(2)}) async-start(), calls=%async_computation.2 | async-start | bytes 1179648 | tf_op jit(solution)/shard_map/while/body/eval_jaxpr/all_gather | solution.py:43
  1092.0 61.8 %all-gather.17.cloned.1.call-start = ((), (), s32[]{:S(2)}) async-start(), calls=%async_computation.2 | async-start | bytes 1179648 | tf_op jit(solution)/shard_map/while/body/eval_jaxpr/all_gather | solution.py:43
  1161.8 61.5 %all-gather.17.cloned.1.call-start = ((), (), s32[]{:S(2)}) async-start(), calls=%async_computation.2 | async-start | bytes 1179648 | tf_op jit(solution)/shard_map/while/body/eval_jaxpr/all_gather | solution.py:43
  1231.3 61.9 %all-gather.17.cloned.1.call-start = ((), (), s32[]{:S(2)}) async-start(), calls=%async_computation.2 | async-start | bytes 1179648 | tf_op jit(solution)/shard_map/while/body/eval_jaxpr/all_gather | solution.py:43
  1301.1 61.5 %all-gather.17.cloned.1.call-start = ((), (), s32[]{:S(2)}) async-start(), calls=%async_computation.2 | async-start | bytes 1179648 | tf_op jit(solution)/shard_map/while/body/eval_jaxpr/all_gather | solution.py:43
  1370.6 61.3 %all-gather.17.cloned.1.call-start = ((), (), s32[]{:S(2)}) async-start(), calls=%async_computation.2 | async-start | bytes 1179648 | tf_op jit(solution)/shard_map/while/body/eval_jaxpr/all_gather | solution.py:43
  1439.9 61.5 %all-gather.17.cloned.1.call-start = ((), (), s32[]{:S(2)}) async-start(), calls=%async_computation.2 | async-start | bytes 1179648 | tf_op jit(solution)/shard_map/while/body/eval_jaxpr/all_gather | solution.py:43
  1509.3 61.8 %all-gather.17.cloned.1.call-start = ((), (), s32[]{:S(2)}) async-start(), calls=%async_computation.2 | async-start | bytes 1179648 | tf_op jit(solution)/shard_map/while/body/eval_jaxpr/all_gather | solution.py:43
  1579.1 61.9 %all-gather.17.cloned.1.call-start = ((), (), s32[]{:S(2)}) async-start(), calls=%async_computation.2 | async-start | bytes 1179648 | tf_op jit(solution)/shard_map/while/body/eval_jaxpr/all_gather | solution.py:43
  1648.9 61.5 %all-gather.17.cloned.1.call-start = ((), (), s32[]{:S(2)}) async-start(), calls=%async_computation.2 | async-start | bytes 1179648 | tf_op jit(solution)/shard_map/while/body/eval_jaxpr/all_gather | solution.py:43
  1718.3 61.8 %all-gather.17.cloned.1.call-start = ((), (), s32[]{:S(2)}) async-start(), calls=%async_computation.2 | async-start | bytes 1179648 | tf_op jit(solution)/shard_map/while/body/eval_jaxpr/all_gather | solution.py:43
  1788.1 61.5 %all-gather.17.cloned.1.call-start = ((), (), s32[]{:S(2)}) async-start(), calls=%async_computation.2 | async-start | bytes 1179648 | tf_op jit(solution)/shard_map/while/body/eval_jaxpr/all_gather | solution.py:43
  1857.5 61.6 %all-gather.17.cloned.1.call-start = ((), (), s32[]{:S(2)}) async-start(), calls=%async_computation.2 | async-start | bytes 1179648 | tf_op jit(solution)/shard_map/while/body/eval_jaxpr/all_gather | solution.py:43
  1927.1 61.5 %all-gather.17.cloned.1.call-start = ((), (), s32[]{:S(2)}) async-start(), calls=%async_computation.2 | async-start | bytes 1179648 | tf_op jit(solution)/shard_map/while/body/eval_jaxpr/all_gather | solution.py:43
  1996.5 61.5 %all-gather.17.cloned.1.call-start = ((), (), s32[]{:S(2)}) async-start(), calls=%async_computation.2 | async-start | bytes 1179648 | tf_op jit(solution)/shard_map/while/body/eval_jaxpr/all_gather | solution.py:43
  2066.0 61.6 %all-gather.17.cloned.1.call-start = ((), (), s32[]{:S(2)}) async-start(), calls=%async_computation.2 | async-start | bytes 1179648 | tf_op jit(solution)/shard_map/while/body/eval_jaxpr/all_gather | solution.py:43
  2135.6 61.9 %all-gather.17.cloned.1.call-start = ((), (), s32[]{:S(2)}) async-start(), calls=%async_computation.2 | async-start | bytes 1179648 | tf_op jit(solution)/shard_map/while/body/eval_jaxpr/all_gather | solution.py:43
  2205.4 61.5 %all-gather.17.cloned.1.call-start = ((), (), s32[]{:S(2)}) async-start(), calls=%async_computation.2 | async-start | bytes 1179648 | tf_op jit(solution)/shard_map/while/body/eval_jaxpr/all_gather | solution.py:43
  2274.9 61.6 %all-gather.17.cloned.1.call-start = ((), (), s32[]{:S(2)}) async-start(), calls=%async_computation.2 | async-start | bytes 1179648 | tf_op jit(solution)/shard_map/while/body/eval_jaxpr/all_gather | solution.py:43
  2344.5 61.6 %all-gather.17.cloned.1.call-start = ((), (), s32[]{:S(2)}) async-start(), calls=%async_computation.2 | async-start | bytes 1179648 | tf_op jit(solution)/shard_map/while/body/eval_jaxpr/all_gather | solution.py:43
  2414.0 61.6 %all-gather.17.cloned.1.call-start = ((), (), s32[]{:S(2)}) async-start(), calls=%async_computation.2 | async-start | bytes 1179648 | tf_op jit(solution)/shard_map/while/body/eval_jaxpr/all_gather | solution.py:43
  2483.6 61.9 %all-gather.17.cloned.1.call-start = ((), (), s32[]{:S(2)}) async-start(), calls=%async_computation.2 | async-start | bytes 1179648 | tf_op jit(solution)/shard_map/while/body/eval_jaxpr/all_gather | solution.py:43
  (77 other events, 5185.1 us)
Sparse Core Ops, SparseCore 0:
  320.4 24.5 all-gather.12
  368.1 19.8 all-gather.16
  394.7 19.8 all-gather.12
  416.0 19.8 all-gather.14
  507.2 19.8 all-gather.16
  533.8 19.8 all-gather.12
  555.3 19.8 all-gather.14
  646.3 19.8 all-gather.16
  694.3 19.8 all-gather.14
  763.8 19.8 all-gather.14
  785.3 19.8 all-gather.16
  812.3 19.8 all-gather.12
  833.8 19.8 all-gather.14
  924.7 19.8 all-gather.16
  973.2 19.8 all-gather.14
  994.5 19.8 all-gather.16
  1021.4 19.8 all-gather.12
  1042.9 19.8 all-gather.14
  1064.2 19.8 all-gather.16
  1133.9 19.8 all-gather.16
  1273.3 19.8 all-gather.16
  1508.4 19.8 all-gather.12
  1551.2 19.8 all-gather.16
  1621.1 19.8 all-gather.16
  1690.5 19.8 all-gather.16
  1738.9 19.8 all-gather.14
  1899.3 19.8 all-gather.16
  1947.4 19.8 all-gather.14
  2086.2 19.8 all-gather.14
  2177.6 19.8 all-gather.16
  2225.7 19.8 all-gather.14
  2364.8 19.8 all-gather.14
  (64 shorter events, 1264.8 us)
where the time goes:
time: 2740 us; the launch traced here: 2730 us
  waiting for transfers between devices  1860 us (68%)
  local copies, waits for them, and re-layouts  550 us (20%)
  matrix products  222 us (8%)
  other arithmetic  86.4 us (3%)
    all_gather x32, waiting for transfers between devices, one_expert(): linear_full = lax.all_gather(linear_part, 'wg', axis=1, tiled=True)  685 us
    all_gather x32, waiting for transfers between devices, one_expert(): down_full = lax.all_gather(down_part, 'wg', axis=0, tiled=True)  613 us
    all_gather x32, waiting for transfers between devices, one_expert(): gelu_full = lax.all_gather(gelu_part, 'wg', axis=1, tiled=True)  553 us
    gather x1, local copies, waits for them, and re-layouts, local_block(): jnp.take(expert_out, slot_of, axis=0).reshape(tok_rows, top_k, d_model)  154 us
    dynamic_slice x96, local copies, waits for them, and re-layouts, local_block(): lax.map(one_expert, (dispatched, w_gelu, w_linear, w_down))  150 us
    dot_general x32, matrix products, one_expert(): return jnp.dot(hidden_act, down_full, preferred_element_type=jnp.float32)  149 us
    gather x2, local copies, waits for them, and re-layouts, route_slots(): slot_token = sort_order[source].reshape(-1) // top_k  90.7 us
    gather x1, local copies, waits for them, and re-layouts, local_block(): jnp.take(normed, slot_token, axis=0).reshape(num_experts, capacity, d_model)  82.1 us
  transfers between devices with their start and end apart: 96, of which 96 were waited for; matrix products, arithmetic and copies ran while one was open for 6% of the time, Pallas kernels for 0%

commit v1 on v0

v1 whole, which is shorter than its diff:
```python
import functools
import jax
import jax.numpy as jnp
from jax import lax
from jax.experimental import pallas as pl
from jax.experimental.pallas import tpu as pltpu
from jax.sharding import PartitionSpec as P

EPS = 1e-5
KG = 0.7978845608028654
KC = KG * 0.044715
SB = 4
LANES = 128
f32, bf16 = jnp.float32, jnp.bfloat16


def gated_act(u, v, gate):
    w = u * (u * u * KC + KG)
    g = u * (0.5 * jnp.tanh(w) + 0.5)
    a = (g * v).astype(bf16).astype(f32)
    ga = jnp.where(gate >= 0, a * gate, 0.0)
    hi = ga.astype(bf16)
    return hi, (ga - hi.astype(f32)).astype(bf16)


def kernel(n, hid, cht, pre, wr, wu_own, wd_own, post, out, fin,
           wu, wd, xr, chs, xb, gts, u0, u1, h0, h1, l0, l1, ys, rel,
           lsem, asem, arem, wsem, wrem, ssem, srem):
    M, D = xb.shape
    NB = wu.shape[0]
    half = NB // 2
    NI = NB // SB
    me = lax.axis_index('wg')
    right, left = lax.rem(me + 2, n), lax.rem(me + n - 2, n)
    mate = me + 1 - 2 * lax.rem(me, 2)

    barrier = pltpu.get_barrier_semaphore()
    for d in (left, right, mate):
        pl.semaphore_signal(barrier, inc=1, device_id={'wg': d}, device_id_type=pl.DeviceIdType.MESH)
    pl.semaphore_wait(barrier, 3)

    def remote(src, dst, ss, rs, dev):
        return pltpu.make_async_remote_copy(src_ref=src, dst_ref=dst, send_sem=ss, recv_sem=rs,
                                            device_id={'wg': dev}, device_id_type=pl.DeviceIdType.MESH)

    hid_a, hid_b = hid.at[pl.ds(0, M)], hid.at[pl.ds(M, M)]

    def gather(k):
        x_src, c_src, dst, dev = (
            (hid_a, cht.at[0], 1, right), (hid_b, cht.at[1], 2, left),
            (xr.at[1], chs.at[1], 4, right), (xr.at[2], chs.at[2], 3, left),
            (hid_a, cht.at[0], 6, left), (hid_b, cht.at[1], 5, right))[k]
        return (remote(c_src, chs.at[dst], asem.at[2 * k], arem.at[2 * k], dev),
                remote(x_src, xr.at[dst], asem.at[2 * k + 1], arem.at[2 * k + 1], dev))

    def weight(k):
        b, r = half // 4, half // 4 * LANES
        return (remote(wu_own.at[pl.ds(k * b, b)], wu.at[pl.ds(half + k * b, b)], wsem.at[2 * k], wrem.at[2 * k], mate),
                remote(wd_own.at[pl.ds(k * r, r)], wd.at[pl.ds(half * LANES + k * r, r)], wsem.at[2 * k + 1], wrem.at[2 * k + 1], mate))

    def partial(k):
        src, dst, dev = (
            (ys.at[1], fin.at[0], left), (ys.at[2], fin.at[1], right),
            (ys.at[3], rel.at[0], left), (ys.at[4], rel.at[1], right),
            (ys.at[1], fin.at[2], left), (ys.at[2], fin.at[3], right))[k]
        return remote(src, dst, ssem.at[k], srem.at[k], dev)

    for k in (0, 1, 5, 4):
        for c in gather(k):
            c.start()
    for k in range(4):
        for c in weight(k):
            c.start()
    local = [pltpu.make_async_copy(hid_a, xr.at[0], lsem.at[0]),
             pltpu.make_async_copy(cht.at[0], chs.at[0], lsem.at[1]),
             pltpu.make_async_copy(wu_own, wu.at[pl.ds(0, half)], lsem.at[2]),
             pltpu.make_async_copy(wd_own, wd.at[pl.ds(0, half * LANES)], lsem.at[3]),
             pltpu.make_async_copy(hid_b, xr.at[7], lsem.at[4]),
             pltpu.make_async_copy(cht.at[1], chs.at[7], lsem.at[5])]
    for c in local:
        c.start()
    for c in local:
        c.wait()

    us, hs, ls = (u0, u1), (h0, h1), (l0, l1)

    def norm(c):
        @pl.loop(0, M // 64)
        def _(t):
            rows = pl.ds(pl.multiple_of(t * 64, 64), 64)
            x = xr[c, rows].astype(f32)
            xb[rows] = (x * lax.rsqrt(jnp.mean(x * x, axis=-1, keepdims=True) + EPS) * pre[...]).astype(bf16)

    def gates(c):
        E = wr.shape[1]
        logits = jnp.dot(xb[...], wr[...], preferred_element_type=f32)
        e = jnp.exp(logits - logits.max(-1, keepdims=True))
        p = e / e.sum(-1, keepdims=True)
        ch = chs[c]
        ids = lax.broadcasted_iota(jnp.int32, (E, M), 0)
        hit = ch[0:1] == ids
        for j in range(1, ch.shape[0]):
            hit = hit | (ch[j:j + 1] == ids)
        eye = jnp.where(lax.broadcasted_iota(jnp.int32, (E, E), 0) == lax.broadcasted_iota(jnp.int32, (E, E), 1), 1.0, 0.0)
        mask = lax.dot_general(jnp.where(hit, 1.0, 0.0).astype(bf16), eye.astype(bf16), (((0,), (0,)), ((), ())),
                               preferred_element_type=f32)
        g = jnp.where(mask > 0.5, p, -1.0)
        low = lax.broadcasted_iota(jnp.int32, (M, LANES), 1) < LANES // 2
        for q in range(E // 2):
            gts[q] = jnp.where(low, g[:, 2 * q:2 * q + 1], g[:, 2 * q + 1:2 * q + 2])

    def slot(c):
        return c - 4 * (c // 5)

    def up(i, p):
        b = lax.rem(i, NI) * SB
        for k in range(SB):
            us[p][:, k * 256:(k + 1) * 256] = jnp.dot(xb[...], wu[b + k], preferred_element_type=f32)

    def act(i, p):
        b = lax.rem(i * SB, half)
        for k in range(SB):
            hi, lo = gated_act(us[p][:, k * 256:k * 256 + 128], us[p][:, k * 256 + 128:(k + 1) * 256], gts[b + k])
            hs[p][:, k * 128:(k + 1) * 128] = hi
            ls[p][:, k * 128:(k + 1) * 128] = lo

    def down(i, p):
        w = wd[pl.ds(pl.multiple_of(lax.rem(i, NI) * (SB * 128), SB * 128), SB * 128)]
        y = ys.at[slot(i // NI)]
        y[...] += jnp.dot(hs[p][...], w, preferred_element_type=f32) + jnp.dot(ls[p][...], w, preferred_element_type=f32)

    norm(0)
    gates(0)
    up(0, 0)
    ys[0] = jnp.zeros((M, D), f32)

    @pl.loop(0, 4 * NI)
    def _(j):
        i = 2 * j
        for k in range(4):
            @pl.when(i == NI // 2 - 2 + 2 * ((k + 1) // 2))
            def _():
                for c in weight(k):
                    c.wait_recv()
        up(i + 1, 1)
        act(i, 0)
        down(i, 0)

        nxt = i + 2
        c = lax.rem(nxt // NI, 8)
        fresh = lax.rem(nxt, NI) == 0

        @pl.when(fresh)
        def _():
            @pl.when(c == 1)
            def _():
                for k in (0, 1):
                    for d in gather(k):
                        d.wait_recv()
                for k in (2, 3):
                    for d in gather(k):
                        d.start()

            @pl.when(c == 3)
            def _():
                for k in (2, 3):
                    for d in gather(k):
                        d.wait_recv()

            @pl.when(c == 5)
            def _():
                for k in (4, 5):
                    for d in gather(k):
                        d.wait_recv()
            norm(c)

        up(nxt, 0)
        act(i + 1, 1)
        down(i + 1, 1)

        @pl.when(fresh & (nxt < 8 * NI))
        def _():
            done = c - 1
            for k in range(4):
                @pl.when(done == 1 + k)
                def _():
                    partial(k).start()
            for k in range(2):
                @pl.when(done == 5 + k)
                def _():
                    partial(2 + k).wait_recv()
                    ys[1 + k] += rel[k]
                    partial(4 + k).start()

                @pl.when(c == 5 + k)
                def _():
                    partial(k).wait_send()

            @pl.when(c == 7)
            def _():
                partial(2).wait_send()
            ys[slot(c)] = jnp.zeros((M, D), f32)
            gates(c)

    def finish(y, a, b, x, o, dst, s):
        ca = pltpu.make_async_copy(fin.at[a], u0, lsem.at[0])
        cb = pltpu.make_async_copy(fin.at[b], u1, lsem.at[1])
        ca.start()
        cb.start()
        ca.wait()
        cb.wait()

        @pl.loop(0, M // 64)
        def _(t):
            rows = pl.ds(pl.multiple_of(t * 64, 64), 64)
            z = ys[y, rows] + u0[rows] + u1[rows]
            r = z * lax.rsqrt(jnp.mean(z * z, axis=-1, keepdims=True) + EPS) * post[...]
            xr[o, rows] = (xr[x, rows].astype(f32) + r).astype(bf16)
        co = pltpu.make_async_copy(xr.at[o], dst, lsem.at[s])
        co.start()
        return co

    partial(0).wait_recv()
    partial(1).wait_recv()
    partial(4).wait_recv()
    ob = finish(3, 1, 2, 7, 5, out.at[pl.ds(M, M)], 2)
    partial(5).wait_recv()
    oa = finish(0, 0, 3, 0, 6, out.at[pl.ds(0, M)], 3)
    for k in range(6):
        for c in gather(k):
            c.wait_send()
    for k in range(4):
        for c in weight(k):
            c.wait_send()
    for k in (3, 4, 5):
        partial(k).wait_send()
    ob.wait()
    oa.wait()


def pair_lanes(w):
    e, d, h = w.shape
    return w.reshape(e // 2, 2, d, h).transpose(0, 2, 1, 3).reshape(e // 2, d, 2 * h)


def solution(mesh):
    n = mesh.shape['wg']

    def local_block(hidden, choice, pre_scale, w_router, w_gelu, w_linear, w_down, post_scale):
        R, D = hidden.shape
        E, _, H = w_gelu.shape
        K = choice.shape[1]
        M = R // 2
        wu_own = jnp.concatenate([pair_lanes(w_gelu), pair_lanes(w_linear)], axis=-1)
        wd_own = w_down.reshape(E * H, D)
        cht = choice.reshape(2, M, K).transpose(0, 2, 1)
        any_spec = pl.BlockSpec(memory_space=pl.ANY)
        vmem = pl.BlockSpec(memory_space=pltpu.VMEM)
        sem = pltpu.SemaphoreType.DMA
        out, _ = pl.pallas_call(
            functools.partial(kernel, n),
            out_shape=[jax.ShapeDtypeStruct((R, D), bf16), jax.ShapeDtypeStruct((4, M, D), f32)],
            in_specs=[any_spec, any_spec, vmem, vmem, any_spec, any_spec, vmem],
            out_specs=[any_spec, any_spec],
            scratch_shapes=[
                pltpu.VMEM((E, D, 4 * H), bf16), pltpu.VMEM((2 * E * H, D), bf16),
                pltpu.VMEM((8, M, D), bf16), pltpu.VMEM((8, K, M), jnp.int32),
                pltpu.VMEM((M, D), bf16), pltpu.VMEM((E // 2, M, LANES), f32),
                pltpu.VMEM((M, 256 * SB), f32), pltpu.VMEM((M, 256 * SB), f32),
                pltpu.VMEM((M, 128 * SB), bf16), pltpu.VMEM((M, 128 * SB), bf16),
                pltpu.VMEM((M, 128 * SB), bf16), pltpu.VMEM((M, 128 * SB), bf16),
                pltpu.VMEM((5, M, D), f32), pltpu.VMEM((2, M, D), f32),
                sem((6,)), sem((12,)), sem((12,)), sem((8,)), sem((8,)), sem((6,)), sem((6,))],
            compiler_params=pltpu.CompilerParams(collective_id=0, has_side_effects=True, vmem_limit_bytes=67043328),
        )(hidden, cht, pre_scale.reshape(1, D), w_router, wu_own, wd_own, post_scale.reshape(1, D))
        return out

    row_spec = P(('dp', 'wg'), None)
    weight_in = P(None, None, 'wg')
    return jax.shard_map(local_block, mesh=mesh, in_specs=(row_spec, row_spec, P(), P(), weight_in, weight_in, P(None, 'wg', None), P()), out_specs=row_spec, check_vma=False)
```

time: 2740 us -> 272 us (0.10)
  waiting for transfers between devices: 1860 us -> 0 us
  local copies, waits for them, and re-layouts: 550 us -> 17.5 us
  Pallas kernels: 0 us -> 246 us
  matrix products: 222 us -> 0 us
  other arithmetic: 86.4 us -> 7.88 us
    all_gather x96 -> x0, waiting for transfers between devices: 1850 us -> none  [the longest x32 685 us: one_expert(): linear_full = lax.all_gather(linear_part, 'wg', axis=1, tiled=True)]
    gather x11 -> x0, local copies, waits for them, and re-layouts: 394 us -> none  [the longest x1 154 us: local_block(): jnp.take(expert_out, slot_of, axis=0).reshape(tok_rows, top_k, d_model)]
    pallas_call x0 -> x1, Pallas kernels: none -> 246 us  [local_block(): pl.pallas_call(functools.partial(kernel, n), out_shape=[jax.ShapeDtypeStr...]
    dot_general x65 -> x0, matrix products: 222 us -> none  [the longest x32 149 us: one_expert(): return jnp.dot(hidden_act, down_full, preferred_element_type=jnp.float32)]
    dynamic_slice x96 -> x0, local copies, waits for them, and re-layouts: 150 us -> none  [local_block(): lax.map(one_expert, (dispatched, w_gelu, w_linear, w_down))]
  transfers between devices with their start and end apart: 96 -> 0, of which waited for: 96 -> 0; matrix products, arithmetic and copies ran while one was open for 6% -> 0% of each run, Pallas kernels for 0% -> 0%
where the time goes in v1:
time: 272 us
  Pallas kernels  246 us (90%)
  local copies, waits for them, and re-layouts  17.5 us (6%)
  other arithmetic  7.88 us (3%)
    pallas_call x1, Pallas kernels, local_block(): pl.pallas_call(functools.partial(kernel, n), out_shape=[jax.ShapeDtypeStr...  246 us
    reshape x2, local copies, waits for them, and re-layouts, pair_lanes(): w.reshape(e // 2, 2, d, h).transpose(0, 2, 1, 3).reshape(e // 2, d, 2 * h)  12.7 us
    concatenate x1, other arithmetic, local_block(): jnp.concatenate([pair_lanes(w_gelu), pair_lanes(w_linear)], axis=-1)  7.88 us

profile of v1, /device:TPU:81, one launch (start us, length us, event | category | flops | bytes accessed | tf_op | source)
XLA Modules:
  0.0 271.8 jit_solution(6025207544127135121)
XLA Ops:
  0.0 1.7 copy.14.wr
  1.7 6.4 %copy.12 = bf16[16,1024,128]{2,1,0:T(8,128)(2,1)} copy(bf16[16,1024,128]{1,2,0:T(8,128)(2,1)} %bitcast.17) | data formatting | bytes 8388608 | tf_op jit(solution)/shard_map/reshape | solution.py:243
  8.1 6.4 %copy.13 = bf16[16,1024,128]{2,1,0:T(8,128)(2,1)} copy(bf16[16,1024,128]{1,2,0:T(8,128)(2,1)} %bitcast.18) | data formatting | bytes 8388608 | tf_op jit(solution)/shard_map/reshape | solution.py:243
  14.4 7.9 %pad_maximum_fusion.wu_own = bf16[16,1024,256]{2,1,0:T(8,128)(2,1)} fusion(bf16[16,1024,128]{2,1,0:T(8,128)(2,1)} %copy.13, bf16[16,1024,128]{2,1,0:T(8,128)(2,1)} %copy.12), kind=kLoop, calls=%fused_computation | loop fusion | flops 16777216 | bytes 16777216 | tf_op jit(solution)/shard_map/concatenate | solution.py:254
  22.3 246.4 %shard_map.82 = (bf16[1024,1024]{1,0:T(8,128)(2,1)}, f32[4,512,1024]{2,1,0:T(8,128)}) custom-call(bf16[1024,1024]{1,0:T(8,128)(2,1)} %hid.1, s32[2,8,512]{2,1,0:T(8,128)} %bitcast.19, f32[1,1024]{1,0:T(1,128)} %bitcast.20, bf16[1024,32]{1,0:T(8,128)(2,1)} %copy.14.wr, bf16[16,1024,256]{2,1,0:T(8,128)(2,1)} %pad_maximum_fusion.wu_own, ...), custom_call_target="tpu_custom_call" | custom-call | tf_op jit(solution)/shard_map/pallas_call | solution.py:260
  268.7 3.1 %copy.16 = bf16[1024,1024]{1,0:T(8,128)(2,1)} copy(bf16[1024,1024]{1,0:T(8,128)(2,1)} %get-tuple-element.6) | data formatting | bytes 4194304

commit v2 on v1

v2 whole, which is shorter than its diff:
```python
import functools
import jax
import jax.numpy as jnp
from jax import lax
from jax.experimental import pallas as pl
from jax.experimental.pallas import tpu as pltpu
from jax.sharding import PartitionSpec as P

EPS = 1e-5
KG = 0.7978845608028654
KC = KG * 0.044715
SB = 4
LANES = 128
f32, bf16 = jnp.float32, jnp.bfloat16


def gated_act(u, v, gate):
    w = u * (u * u * KC + KG)
    g = u * (0.5 * jnp.tanh(w) + 0.5)
    a = (g * v).astype(bf16).astype(f32)
    ga = jnp.where(gate >= 0, a * gate, 0.0)
    hi = ga.astype(bf16)
    return hi, (ga - hi.astype(f32)).astype(bf16)


def kernel(n, hid, cht, pre, wr, wg_own, wl_own, wd_own, post, out, fin,
           wu, wd, xr, chs, xb, gts, sel, u0, u1, h0, h1, l0, l1, ys, rel,
           lsem, asem, arem, vsem, wsem, wrem, ssem, srem):
    M, D = xb.shape
    Q = M // 2
    NB = wu.shape[0]
    half = NB // 2
    NI = NB // SB
    PW = half // 4
    me = lax.axis_index('wg')
    right, left = lax.rem(me + 2, n), lax.rem(me + n - 2, n)
    mate = me + 1 - 2 * lax.rem(me, 2)
    lo_h, hi_h = pl.ds(0, Q), pl.ds(Q, Q)

    barrier = pltpu.get_barrier_semaphore()
    for d in (left, right, mate):
        pl.semaphore_signal(barrier, inc=1, device_id={'wg': d}, device_id_type=pl.DeviceIdType.MESH)
    pl.semaphore_wait(barrier, 3)

    def remote(src, dst, ss, rs, dev):
        return pltpu.make_async_remote_copy(src_ref=src, dst_ref=dst, send_sem=ss, recv_sem=rs,
                                            device_id={'wg': dev}, device_id_type=pl.DeviceIdType.MESH)

    def gather(k, side):
        dev, land, own = ((right, lo_h, (0, 1, 2, 3)), (left, hi_h, (2, 3, 0, 1)))[side]
        if k < 4:
            q = own[k]
            c = (1, 2, 5, 6)[k]
            x_src, c_src, at = hid.at[pl.ds(q * Q, Q)], cht.at[:, pl.ds(q * Q, Q)], land
        else:
            c = k - 1
            x_src, c_src, at = xr.at[k - 3, land], chs.at[k - 3, :, land], (hi_h, lo_h)[side]
        s = 12 * side + 2 * k
        return (remote(c_src, chs.at[c, :, at], asem.at[s], arem.at[s], dev),
                remote(x_src, xr.at[c, at], asem.at[s + 1], arem.at[s + 1], dev))

    def pieces(k, base):
        b, w = pl.ds(base + k * PW, PW), pl.ds((base + k * PW) * LANES, PW * LANES)
        s, v = pl.ds(k * PW, PW), pl.ds(k * PW * LANES, PW * LANES)
        return ((wg_own.at[s], wu.at[b, pl.ds(0, LANES)]), (wl_own.at[s], wu.at[b, pl.ds(LANES, LANES)]),
                (wd_own.at[v], wd.at[w]))

    def weight(k):
        return [remote(src, dst, wsem.at[3 * k + t], wrem.at[3 * k + t], mate)
                for t, (src, dst) in enumerate(pieces(k, half))]

    def load(k):
        return [pltpu.make_async_copy(src, dst, vsem.at[3 * k + t]) for t, (src, dst) in enumerate(pieces(k, 0))]

    def partial(c, side):
        dev, at = ((left, lo_h), (right, hi_h))[side]
        s = c - 4 * (c // 5)
        to = (lo_h, hi_h)[(c - 1) % 2]
        if c < 3:
            dst = fin.at[side, to]
        elif c < 5:
            dst = rel.at[c - 3, at]
        else:
            dst = fin.at[3 - side, to]
        k = 2 * (c - 1) + side
        return remote(ys.at[s, at], dst, ssem.at[k], srem.at[k], dev)

    SIDES = (0, 1)
    for k in range(4):
        for side in SIDES:
            for d in gather(k, side):
                d.start()
    local = [pltpu.make_async_copy(hid.at[pl.ds(0, M)], xr.at[0], lsem.at[0]),
             pltpu.make_async_copy(cht.at[:, pl.ds(0, M)], chs.at[0], lsem.at[1]),
             pltpu.make_async_copy(hid.at[pl.ds(M, M)], xr.at[7], lsem.at[2]),
             pltpu.make_async_copy(cht.at[:, pl.ds(M, M)], chs.at[7], lsem.at[3])]
    for d in local:
        d.start()
    for k in range(4):
        for d in load(k):
            d.start()
    for k in range(4):
        for d in weight(k):
            d.start()
    for d in local:
        d.wait()

    us, hs, ls = (u0, u1), (h0, h1), (l0, l1)
    nt = (((1,), (1,)), ((), ()))

    def norm(c):
        for t in range(2):
            rows = pl.ds(t * Q, Q)
            x = xr[c, rows].astype(f32)
            xb[rows] = (x * lax.rsqrt(jnp.mean(x * x, axis=-1, keepdims=True) + EPS) * pre[...]).astype(bf16)

    E = wr.shape[0]
    iota = lax.broadcasted_iota
    expert_row = lax.rem(iota(jnp.int32, (3 * E, LANES), 0), E)
    for q in range(E // 2):
        lane = iota(jnp.int32, (3 * E, LANES), 1)
        sel[:, q * LANES:(q + 1) * LANES] = jnp.where(expert_row == 2 * q + lane // (LANES // 2), 1.0, 0.0).astype(bf16)

    def gates(c):
        w3 = jnp.concatenate([wr[...]] * 3, axis=0)
        logits = lax.dot_general(xb[...], w3, nt, preferred_element_type=f32)
        lane = iota(jnp.int32, (M, 3 * E), 1)
        e = jnp.exp(logits - logits.max(-1, keepdims=True))
        p = e / jnp.where(lane < E, e, 0.0).sum(-1, keepdims=True)
        ch = chs[c]
        ids = iota(jnp.int32, (E, M), 0)
        hit = ch[0:1] == ids
        for j in range(1, ch.shape[0]):
            hit = hit | (ch[j:j + 1] == ids)
        eye3 = jnp.where(iota(jnp.int32, (E, 3 * E), 0) == lax.rem(iota(jnp.int32, (E, 3 * E), 1), E), 1.0, 0.0)
        mask = lax.dot_general(jnp.where(hit, 1.0, 0.0).astype(bf16), eye3.astype(bf16), (((0,), (0,)), ((), ())),
                               preferred_element_type=f32)
        g = jnp.where(mask > 0.5, p, -1.0)
        top = g.astype(bf16).astype(f32)
        mid = (g - top).astype(bf16).astype(f32)
        g3 = jnp.where(lane < E, top, jnp.where(lane < 2 * E, mid, g - top - mid)).astype(bf16)
        for q in range(0, E // 2, 2):
            t = jnp.dot(g3, sel[:, q * LANES:(q + 2) * LANES], preferred_element_type=f32)
            gts[q] = t[:, :LANES]
            gts[q + 1] = t[:, LANES:]

    def slot(c):
        return c - 4 * (c // 5)

    def up(i, p, ks=range(SB)):
        b = lax.rem(i, NI) * SB
        for k in ks:
            us[p][:, k * 256:(k + 1) * 256] = lax.dot_general(xb[...], wu[b + k], nt, preferred_element_type=f32)

    def act(i, p, ks):
        b = lax.rem(i * SB, half)
        for k in ks:
            hi, lo = gated_act(us[p][:, k * 256:k * 256 + 128], us[p][:, k * 256 + 128:(k + 1) * 256], gts[b + k])
            hs[p][:, k * 128:(k + 1) * 128] = hi
            ls[p][:, k * 128:(k + 1) * 128] = lo

    def down(i, p):
        w = wd[pl.ds(pl.multiple_of(lax.rem(i, NI) * (SB * 128), SB * 128), SB * 128)]
        y = ys.at[slot(i // NI)]
        y[...] += jnp.dot(hs[p][...], w, preferred_element_type=f32) + jnp.dot(ls[p][...], w, preferred_element_type=f32)

    def step(i, p):
        for k in range(SB):
            up(i + 1, 1 - p, (k,))
            act(i, p, (k,))
        down(i, p)

    norm(0)
    gates(0)
    for d in load(0):
        d.wait()
    up(0, 0)
    ys[0] = jnp.zeros((M, D), f32)

    @pl.loop(0, 4 * NI)
    def _(j):
        i = 2 * j

        @pl.when(i == 0)
        def _():
            for k in range(1, 4):
                for d in load(k):
                    d.wait()
        for k in range(4):
            @pl.when(i == NI // 2 - 2 + 2 * ((k + 1) // 2))
            def _():
                for d in weight(k):
                    d.wait_recv()
        step(i, 0)

        nxt = i + 2
        c = lax.rem(nxt // NI, 8)
        fresh = lax.rem(nxt, NI) == 0

        @pl.when(fresh)
        def _():
            for a in range(6):
                @pl.when(c == 1 + a)
                def _():
                    k = (0, 1, 4, 5, 2, 3)[a]
                    for side in SIDES:
                        for d in gather(k, side):
                            d.wait_recv()
                    if k < 2:
                        for side in SIDES:
                            for d in gather(k + 4, side):
                                d.start()
            norm(c)

        step(i + 1, 1)

        @pl.when(fresh & (nxt < 8 * NI))
        def _():
            for a in range(1, 7):
                @pl.when(c - 1 == a)
                def _():
                    if a > 4:
                        for side in SIDES:
                            partial(a - 2, side).wait_recv()
                        ys[a - 4] += rel[a - 5]
                    for side in SIDES:
                        partial(a, side).start()
                if a < 4:
                    @pl.when(c == a + 4)
                    def _():
                        for side in SIDES:
                            partial(a, side).wait_send()
            ys[slot(c)] = jnp.zeros((M, D), f32)
            gates(c)

    def finish(q, p):
        early, late = (0, 2) if q < 2 else (1, 3)
        rows_q = pl.ds((q % 2) * Q, Q)
        buf = us[p]
        ca = pltpu.make_async_copy(fin.at[early, rows_q], buf.at[lo_h], lsem.at[0])
        cb = pltpu.make_async_copy(fin.at[late, rows_q], buf.at[hi_h], lsem.at[1])
        ca.start()
        cb.start()
        ca.wait()
        cb.wait()
        y, x = ((0, 0), (3, 7))[q // 2]
        r0 = (q % 2) * Q

        @pl.loop(0, Q // 64)
        def _(t):
            rows = pl.ds(pl.multiple_of(r0 + t * 64, 64), 64)
            z = ys[y, rows] + buf[pl.ds(pl.multiple_of(t * 64, 64), 64)] + buf[pl.ds(pl.multiple_of(Q + t * 64, 64), 64)]
            r = z * lax.rsqrt(jnp.mean(z * z, axis=-1, keepdims=True) + EPS) * post[...]
            xr[5 + q // 2, rows] = (xr[x, rows].astype(f32) + r).astype(bf16)
        co = pltpu.make_async_copy(xr.at[5 + q // 2, rows_q], out.at[pl.ds(q * Q, Q)], vsem.at[q])
        co.start()
        return co

    for c in (1, 2):
        for side in SIDES:
            partial(c, side).wait_recv()
    for side in SIDES:
        partial(5, side).wait_recv()
    done = [finish(0, 0), finish(2, 1)]
    for side in SIDES:
        partial(6, side).wait_recv()
    done += [finish(1, 0), finish(3, 1)]
    for k in range(6):
        for side in SIDES:
            for d in gather(k, side):
                d.wait_send()
    for k in range(4):
        for d in weight(k):
            d.wait_send()
    for c in (4, 5, 6):
        for side in SIDES:
            partial(c, side).wait_send()
    for d in done:
        d.wait()


def pairs(w):
    e, d, h = w.shape
    return w.transpose(0, 2, 1).reshape(e // 2, 2 * h, d)


def solution(mesh):
    n = mesh.shape['wg']

    def local_block(hidden, choice, pre_scale, w_router, w_gelu, w_linear, w_down, post_scale):
        R, D = hidden.shape
        E, _, H = w_gelu.shape
        K = choice.shape[1]
        M = R // 2
        wd_own = w_down.reshape(E * H, D)
        cht = choice.T
        any_spec = pl.BlockSpec(memory_space=pl.ANY)
        vmem = pl.BlockSpec(memory_space=pltpu.VMEM)
        sem = pltpu.SemaphoreType.DMA
        out, _ = pl.pallas_call(
            functools.partial(kernel, n),
            out_shape=[jax.ShapeDtypeStruct((R, D), bf16), jax.ShapeDtypeStruct((4, M, D), f32)],
            in_specs=[any_spec, any_spec, vmem, vmem, any_spec, any_spec, any_spec, vmem],
            out_specs=[any_spec, any_spec],
            scratch_shapes=[
                pltpu.VMEM((E, 4 * H, D), bf16), pltpu.VMEM((2 * E * H, D), bf16),
                pltpu.VMEM((8, M, D), bf16), pltpu.VMEM((8, K, M), jnp.int32),
                pltpu.VMEM((M, D), bf16), pltpu.VMEM((E // 2, M, LANES), f32), pltpu.VMEM((3 * E, E // 2 * LANES), bf16),
                pltpu.VMEM((M, 256 * SB), f32), pltpu.VMEM((M, 256 * SB), f32),
                pltpu.VMEM((M, 128 * SB), bf16), pltpu.VMEM((M, 128 * SB), bf16),
                pltpu.VMEM((M, 128 * SB), bf16), pltpu.VMEM((M, 128 * SB), bf16),
                pltpu.VMEM((5, M, D), f32), pltpu.VMEM((2, M, D), f32),
                sem((4,)), sem((24,)), sem((24,)), sem((12,)), sem((12,)), sem((12,)), sem((12,)), sem((12,))],
            compiler_params=pltpu.CompilerParams(collective_id=0, has_side_effects=True, vmem_limit_bytes=67043328),
        )(hidden, cht, pre_scale.reshape(1, D), w_router.T, pairs(w_gelu), pairs(w_linear), wd_own, post_scale.reshape(1, D))
        return out

    row_spec = P(('dp', 'wg'), None)
    weight_in = P(None, None, 'wg')
    return jax.shard_map(local_block, mesh=mesh, in_specs=(row_spec, row_spec, P(), P(), weight_in, weight_in, P(None, 'wg', None), P()), out_specs=row_spec, check_vma=False)
```

time: 272 us -> 221 us (0.81)
  Pallas kernels: 246 us -> 217 us
  local copies, waits for them, and re-layouts: 17.5 us -> 3.08 us
  other arithmetic: 7.88 us -> 0 us
    pallas_call x1, Pallas kernels: 246 us -> 217 us  [local_block(): pl.pallas_call(functools.partial(kernel, n), out_shape=[jax.ShapeDtypeStr...]
    reshape x2 -> x0, local copies, waits for them, and re-layouts: 12.7 us -> none  [pair_lanes(): w.reshape(e // 2, 2, d, h).transpose(0, 2, 1, 3).reshape(e // 2, d, 2 * h)]
    concatenate x1 -> x0, other arithmetic: 7.88 us -> none  [local_block(): jnp.concatenate([pair_lanes(w_gelu), pair_lanes(w_linear)], axis=-1)]
where the time goes in v2:
time: 221 us; the launch traced here: 220 us
  Pallas kernels  217 us (98%)
  local copies, waits for them, and re-layouts  3.08 us (1%)
    pallas_call x1, Pallas kernels, local_block(): pl.pallas_call(functools.partial(kernel, n), out_shape=[jax.ShapeDtypeStr...  217 us

profile of v2, /device:TPU:81, one launch (start us, length us, event | category | flops | bytes accessed | tf_op | source)
XLA Modules:
  0.0 220.3 jit_solution(16069894609669944562)
XLA Ops:
  0.0 217.2 %shard_map.82 = (bf16[1024,1024]{1,0:T(8,128)(2,1)}, f32[4,512,1024]{2,1,0:T(8,128)}) custom-call(bf16[1024,1024]{1,0:T(8,128)(2,1)} %hid.1, s32[8,1024]{1,0:T(8,128)} %bitcast.15, f32[1,1024]{1,0:T(1,128)} %bitcast.16, bf16[32,1024]{1,0:T(8,128)(2,1)} %bitcast.14, bf16[16,128,1024]{2,1,0:T(8,128)(2,1)} %bitcast.11, bf16[16,128,1024]{2,1,0:T(8,128)(2,1)} %bitcast.12, ...), custom_call_target="tpu_custom_call" | custom-call | tf_op jit(solution)/shard_map/pallas_call | solution.py:300
  217.2 3.1 %copy.10 = bf16[1024,1024]{1,0:T(8,128)(2,1)} copy(bf16[1024,1024]{1,0:T(8,128)(2,1)} %get-tuple-element.6) | data formatting | bytes 4194304

commit v3 on v2

v3 whole, which is shorter than its diff:
```python
import functools
import jax
import jax.numpy as jnp
from jax import lax
from jax.experimental import pallas as pl
from jax.experimental.pallas import tpu as pltpu
from jax.sharding import PartitionSpec as P

EPS = 1e-5
KG = 0.7978845608028654
KC = KG * 0.044715
SB = 4
LANES = 128
f32, bf16 = jnp.float32, jnp.bfloat16


def gated_act(u, v, gate):
    w = u * (u * u * KC + KG)
    g = u * (0.5 * jnp.tanh(w) + 0.5)
    a = (g * v).astype(bf16).astype(f32)
    ga = jnp.where(gate >= 0, a * gate, 0.0)
    hi = ga.astype(bf16)
    return hi, (ga - hi.astype(f32)).astype(bf16)


def kernel(n, hid, cht, pre, wr, wg_own, wl_own, wd_own, post, out, fin,
           wu, wd, xr, chs, g3, sel, u0, u1, h0, h1, l0, l1, ys, rel, lat,
           lsem, asem, arem, vsem, wsem, wrem, ssem, srem, osem):
    M, D = xr.shape[1:]
    Q = M // 2
    pairs_n = wu.shape[0]
    PS = SB // 2
    NI = pairs_n // PS
    me = lax.axis_index('wg')
    right, left = lax.rem(me + 2, n), lax.rem(me + n - 2, n)
    mate = me + 1 - 2 * lax.rem(me, 2)
    lo_h, hi_h = pl.ds(0, Q), pl.ds(Q, Q)

    barrier = pltpu.get_barrier_semaphore()
    for d in (left, right, mate):
        pl.semaphore_signal(barrier, inc=1, device_id={'wg': d}, device_id_type=pl.DeviceIdType.MESH)
    pl.semaphore_wait(barrier, 3)

    def remote(src, dst, ss, rs, dev):
        return pltpu.make_async_remote_copy(src_ref=src, dst_ref=dst, send_sem=ss, recv_sem=rs,
                                            device_id={'wg': dev}, device_id_type=pl.DeviceIdType.MESH)

    def gather(k, side):
        dev, land, own = ((right, lo_h, (0, 1, 2, 3)), (left, hi_h, (2, 3, 0, 1)))[side]
        if k < 4:
            q = own[k]
            c = (1, 2, 5, 6)[k]
            x_src, c_src, at = hid.at[pl.ds(q * Q, Q)], cht.at[:, pl.ds(q * Q, Q)], land
        else:
            c = k - 1
            x_src, c_src, at = xr.at[k - 3, land], chs.at[k - 3, :, land], (hi_h, lo_h)[side]
        s = 12 * side + 2 * k
        return (remote(c_src, chs.at[c, :, at], asem.at[s], arem.at[s], dev),
                remote(x_src, xr.at[c, at], asem.at[s + 1], arem.at[s + 1], dev))

    def pieces(k, h):
        p = pl.ds(k * PS, PS)
        return ((wg_own.at[p], wu.at[p, h, pl.ds(0, LANES)]), (wl_own.at[p], wu.at[p, h, pl.ds(LANES, LANES)]),
                (wd_own.at[p], wd.at[p, h]))

    def weight(k):
        return [remote(src, dst, wsem.at[3 * k + t], wrem.at[3 * k + t], mate)
                for t, (src, dst) in enumerate(pieces(k, 1))]

    def load(k):
        return [pltpu.make_async_copy(src, dst, vsem.at[3 * k + t]) for t, (src, dst) in enumerate(pieces(k, 0))]

    def arrived(k):
        for d in load(k):
            d.wait()
        for d in weight(k):
            d.wait_recv()

    def partial(c, side, h=0):
        dev, base = ((left, 0), (right, Q))[side]
        s = c - 4 * (c // 5)
        to = ((c - 1) % 2) * Q
        if c < 5:
            at = pl.ds(base, Q)
            dst = fin.at[side, pl.ds(to, Q)] if c < 3 else rel.at[c - 3, at]
        else:
            at = pl.ds(base + h * (Q // 2), Q // 2)
            dst = lat.at[1 - side, pl.ds(to + h * (Q // 2), Q // 2)]
        k = 4 * (c - 1) + 2 * side + h
        return remote(ys.at[s, at], dst, ssem.at[k], srem.at[k], dev)

    SIDES = (0, 1)
    for k in range(4):
        for side in SIDES:
            for d in gather(k, side):
                d.start()
    local = [pltpu.make_async_copy(hid.at[pl.ds(0, M)], xr.at[0], lsem.at[0]),
             pltpu.make_async_copy(cht.at[:, pl.ds(0, M)], chs.at[0], lsem.at[1]),
             pltpu.make_async_copy(hid.at[pl.ds(M, M)], xr.at[7], lsem.at[2]),
             pltpu.make_async_copy(cht.at[:, pl.ds(M, M)], chs.at[7], lsem.at[3])]
    for d in local:
        d.start()
    for k in range(NI):
        for d in load(k) + weight(k):
            d.start()
    E = wr.shape[0]
    iota = lax.broadcasted_iota
    expert_row = lax.rem(iota(jnp.int32, (3 * E, LANES), 0), E)
    for q in range(E // 2):
        lane = iota(jnp.int32, (3 * E, LANES), 1)
        sel[q // PS, :, (q % PS) * LANES:(q % PS + 1) * LANES] = jnp.where(
            expert_row == 2 * q + lane // (LANES // 2), 1.0, 0.0).astype(bf16)

    for d in local:
        d.wait()

    again = [pltpu.make_async_copy(hid.at[pl.ds(k * M, M)], xr.at[1 + k], lsem.at[2 * k]) for k in range(2)]
    us, hs, ls = (u0, u1), (h0, h1), (l0, l1)
    nt = (((1,), (1,)), ((), ()))

    def norm(c):
        for t in range(2):
            rows = pl.ds(t * Q, Q)
            x = xr[c, rows].astype(f32)
            xr[c, rows] = (x * lax.rsqrt(jnp.mean(x * x, axis=-1, keepdims=True) + EPS) * pre[...]).astype(bf16)

    def gates(c):
        w3 = jnp.concatenate([wr[...]] * 3, axis=0)
        logits = lax.dot_general(xr[c], w3, nt, preferred_element_type=f32)
        lane = iota(jnp.int32, (M, 3 * E), 1)
        e = jnp.exp(logits - logits.max(-1, keepdims=True))
        p = e / jnp.where(lane < E, e, 0.0).sum(-1, keepdims=True)
        ch = chs[c]
        ids = iota(jnp.int32, (E, M), 0)
        hit = ch[0:1] == ids
        for j in range(1, ch.shape[0]):
            hit = hit | (ch[j:j + 1] == ids)
        eye3 = jnp.where(iota(jnp.int32, (E, 3 * E), 0) == lax.rem(iota(jnp.int32, (E, 3 * E), 1), E), 1.0, 0.0)
        mask = lax.dot_general(jnp.where(hit, 1.0, 0.0).astype(bf16), eye3.astype(bf16), (((0,), (0,)), ((), ())),
                               preferred_element_type=f32)
        g = jnp.where(mask > 0.5, p, -1.0)
        top = g.astype(bf16).astype(f32)
        mid = (g - top).astype(bf16).astype(f32)
        g3[...] = jnp.where(lane < E, top, jnp.where(lane < 2 * E, mid, g - top - mid)).astype(bf16)

    def slot(c):
        return c - 4 * (c // 5)

    def up(i, p, ks):
        b = lax.rem(i, NI) * PS
        x = xr.at[lax.rem(i // NI, 8)]
        for k in ks:
            us[p][:, k * 256:(k + 1) * 256] = lax.dot_general(x[...], wu[b + k // 2, k % 2], nt, preferred_element_type=f32)

    def act(p, ks, gate):
        for k in ks:
            hi, lo = gated_act(us[p][:, k * 256:k * 256 + 128], us[p][:, k * 256 + 128:(k + 1) * 256],
                               gate[:, (k // 2) * LANES:(k // 2 + 1) * LANES])
            hs[p][:, k * 128:(k + 1) * 128] = hi
            ls[p][:, k * 128:(k + 1) * 128] = lo

    def down(i, p, t):
        r = PS * LANES
        w = wd[pl.ds(lax.rem(i, NI) * PS + t * (PS // 2), PS // 2)].reshape(r, D)
        y = ys.at[slot(i // NI)]
        cols = pl.ds(t * r, r)
        old = y[...]
        if t == 0:
            old = jnp.where(lax.rem(i, NI) == 0, 0.0, old)
        y[...] = old + (jnp.dot(hs[p][:, cols], w, preferred_element_type=f32) + jnp.dot(ls[p][:, cols], w, preferred_element_type=f32))

    def step(i, p):
        gate = jnp.dot(g3[...], sel[lax.rem(i, NI)], preferred_element_type=f32)
        act(p, range(SB // 2), gate)
        up(i + 1, 1 - p, range(SB // 2))
        act(p, range(SB // 2, SB), gate)
        down(i, p, 0)
        up(i + 1, 1 - p, range(SB // 2, SB))
        down(i, p, 1)

    norm(0)
    gates(0)
    arrived(0)
    up(0, 0, range(SB))

    @pl.loop(0, 4 * NI)
    def _(j):
        i = 2 * j

        for k in range(1, NI, 2):
            @pl.when(i == k - 1)
            def _():
                arrived(k)
        step(i, 0)

        nxt = i + 2
        for k in range(2, NI, 2):
            @pl.when(nxt == k)
            def _():
                arrived(k)
        c = lax.rem(nxt // NI, 8)
        fresh = lax.rem(nxt, NI) == 0

        @pl.when(fresh)
        def _():
            for a in range(6):
                @pl.when(c == 1 + a)
                def _():
                    for side in SIDES:
                        for d in gather((0, 1, 4, 5, 2, 3)[a], side):
                            d.wait_recv()

            @pl.when((c != 3) & (c != 4))
            def _():
                norm(c)
            for a in range(2):
                @pl.when(c == 1 + a)
                def _():
                    for side in SIDES:
                        for d in gather(a + 4, side):
                            d.start()

            @pl.when(c == 5)
            def _():
                for k in (4, 5):
                    for side in SIDES:
                        for d in gather(k, side):
                            d.wait_send()
                for d in again:
                    d.start()

        step(i + 1, 1)

        @pl.when(fresh & (nxt < 8 * NI))
        def _():
            for a in range(1, 7):
                @pl.when(c - 1 == a)
                def _():
                    if a > 4:
                        for side in SIDES:
                            partial(a - 2, side).wait_recv()
                        ys[a - 4] += rel[a - 5]
                    for h in range(1 + a // 5):
                        for side in SIDES:
                            partial(a, side, h).start()
                if a < 4:
                    @pl.when(c == a + 4)
                    def _():
                        for side in SIDES:
                            partial(a, side).wait_send()
            gates(c)

    BLK = Q // 2
    staged = {}

    def stage(t, dst, src, k):
        d = pltpu.make_async_copy(src, dst, vsem.at[k])
        d.start()
        staged[t] = d

    def early(q):
        return fin.at[q // 2, pl.ds((q % 2) * Q, Q)]

    def home(q):
        return (0, 3)[q // 2], 1 + q // 2, (q % 2) * Q

    def finish(q, h):
        y, x, r0 = home(q)
        rows = pl.ds(r0 + h * BLK, BLK)
        z = ys[y, rows] + lat[q // 2, rows]
        r = z * lax.rsqrt(jnp.mean(z * z, axis=-1, keepdims=True) + EPS) * post[...]
        xr[5 + q // 2, rows] = (xr[x, rows].astype(f32) + r).astype(bf16)
        co = pltpu.make_async_copy(xr.at[5 + q // 2, rows], out.at[pl.ds(q * Q + h * BLK, BLK)], osem.at[2 * q + h])
        co.start()
        return co

    for c in (1, 2):
        for side in SIDES:
            partial(c, side).wait_recv()
    bufs = {0: u0.at[lo_h, pl.ds(0, D)], 2: u0.at[hi_h, pl.ds(0, D)], 1: u1.at[lo_h, pl.ds(0, D)], 3: u1.at[hi_h, pl.ds(0, D)]}
    for q in range(4):
        stage(q, bufs[q], early(q), q)
    for q in range(4):
        staged[q].wait()
        y, x, r0 = home(q)
        ys[y, pl.ds(r0, Q)] += bufs[q][...]
    for d in again:
        d.wait()
    done = []
    for half_q, c in ((0, 5), (1, 6)):
        for h in range(2):
            for side in SIDES:
                partial(c, side, h).wait_recv()
            for q in (half_q, half_q + 2):
                done.append(finish(q, h))
    for k in range(4):
        for side in SIDES:
            for d in gather(k, side):
                d.wait_send()
    for k in range(NI):
        for d in weight(k):
            d.wait_send()
    for c in (4, 5, 6):
        for h in range(1 + c // 5):
            for side in SIDES:
                partial(c, side, h).wait_send()
    for d in done:
        d.wait()


def pairs(w):
    e, d, h = w.shape
    return w.transpose(0, 2, 1).reshape(e // 2, 2 * h, d)


def solution(mesh):
    n = mesh.shape['wg']

    def local_block(hidden, choice, pre_scale, w_router, w_gelu, w_linear, w_down, post_scale):
        R, D = hidden.shape
        E, _, H = w_gelu.shape
        K = choice.shape[1]
        M = R // 2
        wd_own = w_down.reshape(E // 2, 2 * H, D)
        cht = choice.T
        any_spec = pl.BlockSpec(memory_space=pl.ANY)
        vmem = pl.BlockSpec(memory_space=pltpu.VMEM)
        sem = pltpu.SemaphoreType.DMA
        out, _ = pl.pallas_call(
            functools.partial(kernel, n),
            out_shape=[jax.ShapeDtypeStruct((R, D), bf16), jax.ShapeDtypeStruct((2, M, D), f32)],
            in_specs=[any_spec, any_spec, vmem, vmem, any_spec, any_spec, any_spec, vmem],
            out_specs=[any_spec, any_spec],
            scratch_shapes=[
                pltpu.VMEM((E // 2, 2, 4 * H, D), bf16), pltpu.VMEM((E // 2, 2, 2 * H, D), bf16),
                pltpu.VMEM((8, M, D), bf16), pltpu.VMEM((8, K, M), jnp.int32),
                pltpu.VMEM((M, 3 * E), bf16), pltpu.VMEM((E // SB, 3 * E, SB // 2 * LANES), bf16),
                pltpu.VMEM((M, 256 * SB), f32), pltpu.VMEM((M, 256 * SB), f32),
                pltpu.VMEM((M, 128 * SB), bf16), pltpu.VMEM((M, 128 * SB), bf16),
                pltpu.VMEM((M, 128 * SB), bf16), pltpu.VMEM((M, 128 * SB), bf16),
                pltpu.VMEM((5, M, D), f32), pltpu.VMEM((2, M, D), f32), pltpu.VMEM((2, M, D), f32),
                sem((4,)), sem((24,)), sem((24,)), sem((3 * E // SB,)), sem((3 * E // SB,)), sem((3 * E // SB,)), sem((24,)), sem((24,)), sem((8,))],
            compiler_params=pltpu.CompilerParams(collective_id=0, has_side_effects=True, vmem_limit_bytes=67043328),
        )(hidden, cht, pre_scale.reshape(1, D), w_router.T, pairs(w_gelu), pairs(w_linear), wd_own, post_scale.reshape(1, D))
        return out

    row_spec = P(('dp', 'wg'), None)
    weight_in = P(None, None, 'wg')
    return jax.shard_map(local_block, mesh=mesh, in_specs=(row_spec, row_spec, P(), P(), weight_in, weight_in, P(None, 'wg', None), P()), out_specs=row_spec, check_vma=False)
```

time: 221 us -> 215 us (0.973)
  Pallas kernels: 217 us -> 211 us
    pallas_call x1, Pallas kernels: 217 us -> 211 us  [local_block(): pl.pallas_call(functools.partial(kernel, n), out_shape=[jax.ShapeDtypeStr...]
where the time goes in v3:
time: 215 us
  Pallas kernels  211 us (98%)
  local copies, waits for them, and re-layouts  3.08 us (1%)
    pallas_call x1, Pallas kernels, local_block(): pl.pallas_call(functools.partial(kernel, n), out_shape=[jax.ShapeDtypeStr...  211 us

profile of v3, /device:TPU:81, one launch (start us, length us, event | category | flops | bytes accessed | tf_op | source)
XLA Modules:
  0.0 214.5 jit_solution(711789909609550830)
XLA Ops:
  0.0 211.4 %shard_map.82 = (bf16[1024,1024]{1,0:T(8,128)(2,1)}, f32[2,512,1024]{2,1,0:T(8,128)}) custom-call(bf16[1024,1024]{1,0:T(8,128)(2,1)} %hid.1, s32[8,1024]{1,0:T(8,128)} %bitcast.15, f32[1,1024]{1,0:T(1,128)} %bitcast.16, bf16[32,1024]{1,0:T(8,128)(2,1)} %bitcast.14, bf16[16,128,1024]{2,1,0:T(8,128)(2,1)} %bitcast.11, bf16[16,128,1024]{2,1,0:T(8,128)(2,1)} %bitcast.12, ...), custom_call_target="tpu_custom_call" | custom-call | tf_op jit(solution)/shard_map/pallas_call | solution.py:329
  211.4 3.1 %copy.10 = bf16[1024,1024]{1,0:T(8,128)(2,1)} copy(bf16[1024,1024]{1,0:T(8,128)(2,1)} %get-tuple-element.6) | data formatting | bytes 4194304

commit v4 on v3

--- a/solution.py
+++ b/solution.py
@@ -45,18 +45,28 @@
         return pltpu.make_async_remote_copy(src_ref=src, dst_ref=dst, send_sem=ss, recv_sem=rs,
                                             device_id={'wg': dev}, device_id_type=pl.DeviceIdType.MESH)
 
-    def gather(k, side):
+    def gather_at(k, side):
         dev, land, own = ((right, lo_h, (0, 1, 2, 3)), (left, hi_h, (2, 3, 0, 1)))[side]
         if k < 4:
             q = own[k]
             c = (1, 2, 5, 6)[k]
-            x_src, c_src, at = hid.at[pl.ds(q * Q, Q)], cht.at[:, pl.ds(q * Q, Q)], land
+            x_src, c_src, at = hid.at[pl.ds(q * Q, Q)], chs.at[(0, 7)[q // 2], :, pl.ds((q % 2) * Q, Q)], land
         else:
             c = k - 1
             x_src, c_src, at = xr.at[k - 3, land], chs.at[k - 3, :, land], (hi_h, lo_h)[side]
         s = 12 * side + 2 * k
-        return (remote(c_src, chs.at[c, :, at], asem.at[s], arem.at[s], dev),
-                remote(x_src, xr.at[c, at], asem.at[s + 1], arem.at[s + 1], dev))
+        return c_src, x_src, c, at, s, dev
+
+    def gather_ids(k, side):
+        c_src, _, c, at, s, dev = gather_at(k, side)
+        return remote(c_src, chs.at[c, :, at], asem.at[s], arem.at[s], dev)
+
+    def gather_rows(k, side):
+        _, x_src, c, at, s, dev = gather_at(k, side)
+        return remote(x_src, xr.at[c, at], asem.at[s + 1], arem.at[s + 1], dev)
+
+    def gather(k, side):
+        return gather_ids(k, side), gather_rows(k, side)
 
     def pieces(k, h):
         p = pl.ds(k * PS, PS)
@@ -90,19 +100,22 @@
         return remote(ys.at[s, at], dst, ssem.at[k], srem.at[k], dev)
 
     SIDES = (0, 1)
-    for k in range(4):
-        for side in SIDES:
-            for d in gather(k, side):
-                d.start()
+    for side in SIDES:
+        gather_rows(0, side).start()
+    chs[0] = cht[:, :M].astype(f32).astype(bf16)
+    chs[7] = cht[:, M:].astype(f32).astype(bf16)
     local = [pltpu.make_async_copy(hid.at[pl.ds(0, M)], xr.at[0], lsem.at[0]),
-             pltpu.make_async_copy(cht.at[:, pl.ds(0, M)], chs.at[0], lsem.at[1]),
-             pltpu.make_async_copy(hid.at[pl.ds(M, M)], xr.at[7], lsem.at[2]),
-             pltpu.make_async_copy(cht.at[:, pl.ds(M, M)], chs.at[7], lsem.at[3])]
+             pltpu.make_async_copy(hid.at[pl.ds(M, M)], xr.at[7], lsem.at[2])]
     for d in local:
         d.start()
     for k in range(NI):
         for d in load(k) + weight(k):
             d.start()
+    for k in range(4):
+        for side in SIDES:
+            gather_ids(k, side).start()
+            if k:
+                gather_rows(k, side).start()
     E = wr.shape[0]
     iota = lax.broadcasted_iota
     expert_row = lax.rem(iota(jnp.int32, (3 * E, LANES), 0), E)
@@ -130,8 +143,8 @@
         lane = iota(jnp.int32, (M, 3 * E), 1)
         e = jnp.exp(logits - logits.max(-1, keepdims=True))
         p = e / jnp.where(lane < E, e, 0.0).sum(-1, keepdims=True)
-        ch = chs[c]
-        ids = iota(jnp.int32, (E, M), 0)
+        ch = chs[c].astype(f32)
+        ids = iota(jnp.int32, (E, M), 0).astype(f32)
         hit = ch[0:1] == ids
         for j in range(1, ch.shape[0]):
             hit = hit | (ch[j:j + 1] == ids)
@@ -308,6 +321,19 @@
         d.wait()
 
 
+def move(src, dst, buf, si, so):
+    n, r = buf.shape[:2]
+    ins = [pltpu.make_async_copy(src.at[pl.ds(k * r, r)], buf.at[k], si.at[k]) for k in range(n)]
+    outs = [pltpu.make_async_copy(buf.at[k], dst.at[pl.ds(k * r, r)], so.at[k]) for k in range(n)]
+    for d in ins:
+        d.start()
+    for k in range(n):
+        ins[k].wait()
+        outs[k].start()
+    for d in outs:
+        d.wait()
+
+
 def pairs(w):
     e, d, h = w.shape
     return w.transpose(0, 2, 1).reshape(e // 2, 2 * h, d)
@@ -329,11 +355,11 @@
         out, _ = pl.pallas_call(
             functools.partial(kernel, n),
             out_shape=[jax.ShapeDtypeStruct((R, D), bf16), jax.ShapeDtypeStruct((2, M, D), f32)],
-            in_specs=[any_spec, any_spec, vmem, vmem, any_spec, any_spec, any_spec, vmem],
+            in_specs=[any_spec, vmem, vmem, vmem, any_spec, any_spec, any_spec, vmem],
             out_specs=[any_spec, any_spec],
             scratch_shapes=[
                 pltpu.VMEM((E // 2, 2, 4 * H, D), bf16), pltpu.VMEM((E // 2, 2, 2 * H, D), bf16),
-                pltpu.VMEM((8, M, D), bf16), pltpu.VMEM((8, K, M), jnp.int32),
+                pltpu.VMEM((8, M, D), bf16), pltpu.VMEM((8, K, M), bf16),
                 pltpu.VMEM((M, 3 * E), bf16), pltpu.VMEM((E // SB, 3 * E, SB // 2 * LANES), bf16),
                 pltpu.VMEM((M, 256 * SB), f32), pltpu.VMEM((M, 256 * SB), f32),
                 pltpu.VMEM((M, 128 * SB), bf16), pltpu.VMEM((M, 128 * SB), bf16),
@@ -342,7 +368,10 @@
                 sem((4,)), sem((24,)), sem((24,)), sem((3 * E // SB,)), sem((3 * E // SB,)), sem((3 * E // SB,)), sem((24,)), sem((24,)), sem((8,))],
             compiler_params=pltpu.CompilerParams(collective_id=0, has_side_effects=True, vmem_limit_bytes=67043328),
         )(hidden, cht, pre_scale.reshape(1, D), w_router.T, pairs(w_gelu), pairs(w_linear), wd_own, post_scale.reshape(1, D))
-        return out
+        parts = 8
+        return pl.pallas_call(
+            move, out_shape=jax.ShapeDtypeStruct((R, D), bf16), in_specs=[any_spec], out_specs=any_spec,
+            scratch_shapes=[pltpu.VMEM((parts, R // parts, D), bf16), sem((parts,)), sem((parts,))])(out)
 
     row_spec = P(('dp', 'wg'), None)
     weight_in = P(None, None, 'wg')

time: 215 us -> 214 us (level)
  local copies, waits for them, and re-layouts: 3.08 us -> 0 us
    unnamed x1 -> x0, local copies, waits for them, and re-layouts: 3.08 us -> none
    pallas_call x0 -> x1, Pallas kernels: none -> 2.39 us  [local_block(): pl.pallas_call(move, out_shape=jax.ShapeDtypeStruct((R, D), bf16), in_spe...]
where the time goes in v4:
time: 214 us; the launch traced here: 213 us
  Pallas kernels  213 us (100%)
    pallas_call x1, Pallas kernels, local_block(): pl.pallas_call(functools.partial(kernel, n), out_shape=[jax.ShapeDtypeStr...  211 us

profile of v4, /device:TPU:81, one launch (start us, length us, event | category | flops | bytes accessed | tf_op | source)
XLA Modules:
  0.0 213.4 jit_solution(6042409082994494173)
XLA Ops:
  0.0 210.9 %shard_map.82 = (bf16[1024,1024]{1,0:T(8,128)(2,1)}, f32[2,512,1024]{2,1,0:T(8,128)}) custom-call(bf16[1024,1024]{1,0:T(8,128)(2,1)} %hid.1, s32[8,1024]{1,0:T(8,128)} %bitcast.15, f32[1,1024]{1,0:T(1,128)} %bitcast.16, bf16[32,1024]{1,0:T(8,128)(2,1)} %bitcast.14, bf16[16,128,1024]{2,1,0:T(8,128)(2,1)} %bitcast.11, bf16[16,128,1024]{2,1,0:T(8,128)(2,1)} %bitcast.12, ...), custom_call_target="tpu_custom_call" | custom-call | tf_op jit(solution)/shard_map/pallas_call | solution.py:355
  211.0 2.4 %shard_map.83 = bf16[1024,1024]{1,0:T(8,128)(2,1)} custom-call(bf16[1024,1024]{1,0:T(8,128)(2,1)} %get-tuple-element.6.src), custom_call_target="tpu_custom_call" | custom-call | tf_op jit(solution)/shard_map/pallas_call | solution.py:372
